TPU v7x, 32 devices: a whole 2x2x4 slice. The times are simulated.
32 devices in a mesh: row: 8 (over z, core), col: 4 (over y, x).
Axes of the slice: x: 2, y: 2, z: 4, core: 2. Of those that a mesh axis runs over, the one named last changes fastest.
Arguments:
- loadings: bfloat16 [8, 32768, 1024], P(None, 'row', 'col'), may hold values from -6 to 6
- weights: bfloat16 [8, 32768, 512], P(None, 'row', 'col'), may hold values from -0.03125 to 0.03125
- specific: float32 [8, 32768], P(None, 'row'), may hold values from 0.2 to 5
- factor_cov: float32 [8, 1024, 1024], P(None, 'col'), may hold values from -0.001953125 to 0.0048828125, as said below
Outputs:
- portfolio_cov: float32 [8, 512, 512], P(None, 'row', 'col')
Inputs may be any that keep to these rules, and one draw needn't show every extreme that they name: `factor_cov`: each day's matrix is a symmetric positive definite factor covariance of order 1024.
All inputs are finite; a program needn't handle non-finite values.
Results may differ from a plain program's by a relative error of at most 0.0003.
Values may be sent and summed in bfloat16 or wider, within the bound.
A program may use at most 128 MiB of HBM per device.

v0:
```python
import jax
import jax.numpy as jnp
from jax import lax
from jax.sharding import PartitionSpec as P


def shards(loadings, weights, specific, factor_cov):
    factor_cols = loadings.shape[2]
    port_cols = weights.shape[2]
    total_ports = port_cols * lax.axis_size("col")
    port_rows = total_ports // lax.axis_size("row")
    row_start = lax.axis_index("row") * port_rows
    weighted = (specific[:, :, None] * weights.astype(jnp.float32)).astype(jnp.bfloat16)
    fragment = lax.all_gather(weights, "col", axis=2, tiled=True)
    exposure_part = jnp.einsum(
        "dar,dap->drp", loadings, fragment, preferred_element_type=jnp.float32
    )
    specific_term = jnp.einsum(
        "dak,dap->dkp", weighted, fragment, preferred_element_type=jnp.float32
    )
    joined = jnp.concatenate([exposure_part, specific_term], axis=1)
    exposure = lax.psum(joined[:, :factor_cols, :], "row")
    specific_block = lax.psum_scatter(
        joined[:, factor_cols:, :], "row", scatter_dimension=2, tiled=True
    )
    exposure_rows = lax.dynamic_slice_in_dim(exposure, row_start, port_rows, 2)
    left_part = jnp.einsum(
        "dri,drs->dis", exposure_rows, factor_cov, precision=lax.Precision.HIGHEST
    )
    left = lax.psum(left_part, "col")
    exposure_cols = lax.all_to_all(exposure, "col", split_axis=2, concat_axis=1, tiled=True)
    factor_block = jnp.einsum("dir,drk->dik", left, exposure_cols, precision=lax.Precision.HIGHEST)
    return factor_block + jnp.swapaxes(specific_block, 1, 2)


def solution(mesh):
    in_specs = (P(None, "row", "col"), P(None, "row", "col"), P(None, "row"), P(None, "col", None))
    out_specs = P(None, "row", "col")
    return jax.shard_map(shards, mesh=mesh, in_specs=in_specs, out_specs=out_specs, check_vma=False)
```

profile of v0, /device:TPU:0, one launch (start us, length us, event | category | flops | bytes accessed | tf_op | source)
XLA Modules:
  0.0 558.4 jit_solution(18040227865551506382)
XLA Ops:
  6.5 0.0 all-gather.2.cloned.1.call-start
  6.5 0.7 all-gather.2.cloned.1.call-update
  7.3 0.0 copy-start
  7.3 0.0 all-reduce.3.cloned.1.call-start
  7.3 301.6 %all-gather.2.cloned.1.call-done = bf16[8,4096,512]{2,1,0:T(8,128)(2,1)} async-done(((bf16[8,4096,128]{2,1,0:T(8,128)(2,1)}), bf16[8,4096,512]{2,1,0:T(8,128)(2,1)}) %all-gather.2.cloned.1.call-update) | async-done | bytes 33554448 | tf_op jit(solution)/shard_map/all_gather | solution.py:14
  308.9 21.1 %fusion.5 = f32[8,256,512]{2,1,0:T(8,128)} fusion(bf16[8,4096,256]{2,1,0:T(8,128)(2,1)} %param.4, bf16[8,4096,512]{2,1,0:T(8,128)(2,1)} %all-gather.2.cloned.1.call-done), kind=kOutput, calls=%fused_computation.7 | convolution fusion | flops 8589934592 | bytes 54525952 | tf_op jit(solution)/shard_map/dar,dap->drp/dot_general | solution.py:15
  329.9 0.0 all-reduce.3.cloned.1.call-update
  330.0 0.0 reduce-scatter.2.cloned.1.call-start
  330.0 0.0 copy-done
  330.0 21.5 %fusion = f32[8,128,512]{1,2,0:T(8,128)} fusion(bf16[8,4096,512]{2,1,0:T(8,128)(2,1)} %all-gather.2.cloned.1.call-done, bf16[8,4096,128]{2,1,0:T(8,128)(2,1)} %param.5, f32[8,4096]{1,0:T(8,128)S(1)} %copy-done), kind=kOutput, calls=%fused_computation.1 | convolution fusion | flops 4307550208 | bytes 44171264 | tf_op jit(solution)/shard_map/dak,dap->dkp/dot_general | solution.py:18
  351.5 0.0 reduce-scatter.2.cloned.1.call-update
  351.5 75.1 %all-reduce.3.cloned.1.call-done = f32[8,256,512]{2,1,0:T(8,128)} async-done(((f32[8,256,512]{2,1,0:T(8,128)}), f32[8,256,512]{2,1,0:T(8,128)}) %all-reduce.3.cloned.1.call-update) | async-done | bytes 4194320 | tf_op jit(solution)/shard_map/psum | solution.py:22
  426.6 5.5 copy.9
  432.1 5.0 all-to-all-start
  437.1 0.2 all-reduce.5.cloned.1.call-start
  437.3 10.4 %fusion.2 = f32[8,64,1024]{2,1,0:T(8,128)} fusion(f32[8,256,1024]{2,1,0:T(8,128)} %param.7, f32[8,256,512]{2,1,0:T(8,128)} %all-reduce.3.cloned.1.call-done, s32[]{:T(128)S(6)} %select_n.3), kind=kOutput, calls=%fused_computation.4 | convolution fusion | flops 1610612736 | bytes 11534340 | tf_op jit(solution)/shard_map/dri,drs->dis/dot_general | solution.py:27
  447.7 0.0 all-reduce.5.cloned.1.call-update
  447.7 47.9 %all-to-all-done = f32[8,256,512]{1,0,2:T(8,128)} async-done(((f32[8,256,512]{1,0,2:T(8,128)}), f32[8,256,512]{1,0,2:T(8,128)}, u32[]{:S(2)}, u32[]{:S(2)}) %all-to-all-start) | async-done | bytes 4194336 | tf_op jit(solution)/shard_map/all_to_all | solution.py:31
  495.6 5.3 copy.10
  500.9 0.0 reduce-scatter.2.cloned.1.call-done
  500.9 44.7 %all-reduce.5.cloned.1.call-done = f32[8,64,1024]{2,1,0:T(8,128)} async-done(((f32[8,64,1024]{2,1,0:T(8,128)}), f32[8,64,1024]{2,1,0:T(8,128)}) %all-reduce.5.cloned.1.call-update) | async-done | bytes 2097168 | tf_op jit(solution)/shard_map/psum | solution.py:30
  545.7 6.2 %convolution_add_fusion = f32[8,64,128]{2,1,0:T(8,128)} fusion(f32[8,64,1024]{2,1,0:T(8,128)} %all-reduce.5.cloned.1.call-done, f32[8,1024,128]{2,1,0:T(8,128)} %bitcast.12, f32[8,128,64]{1,2,0:T(8,128)} %reduce-scatter.2.cloned.1.call-done), kind=kOutput, calls=%fused_computation.3 | convolution fusion | flops 805371904 | bytes 6815744 | tf_op jit(solution)/shard_map/dir,drk->dik/dot_general | solution.py:32
Async XLA Ops:
  6.5 302.3 %all-gather.2.cloned.1.call-start = ((), (), s32[]{:S(2)}) async-start(), calls=%async_computation.2 | async-start | bytes 41943040 | tf_op jit(solution)/shard_map/all_gather | solution.py:14
  7.3 322.8 %copy-start = (f32[8,4096]{1,0:T(8,128)S(1)}, f32[8,4096]{1,0:T(8,128)}, u32[]{:S(2)}) copy-start(f32[8,4096]{1,0:T(8,128)} %param.6) | copy-start | bytes 393220
  7.3 419.3 %all-reduce.3.cloned.1.call-start = ((), (), s32[]{:S(2)}) async-start(), calls=%async_computation.3 | async-start | bytes 8388608 | tf_op jit(solution)/shard_map/psum | solution.py:22
  330.0 171.0 %reduce-scatter.2.cloned.1.call-start = ((), (), s32[]{:S(2)}) async-start(), calls=%async_computation.5 | async-start | bytes 2359296 | tf_op jit(solution)/shard_map/reduce_scatter | solution.py:23
  432.1 63.5 %all-to-all-start = ((f32[8,256,512]{1,0,2:T(8,128)}), f32[8,256,512]{1,0,2:T(8,128)}, u32[]{:S(2)}, u32[]{:S(2)}) async-start(f32[8,256,512]{1,0,2:T(8,128)} %copy.9), calls=%async_computation | async-start | bytes 8388608 | tf_op jit(solution)/shard_map/all_to_all | solution.py:31
  437.1 108.6 %all-reduce.5.cloned.1.call-start = ((), (), s32[]{:S(2)}) async-start(), calls=%async_computation.4 | async-start | bytes 4194304 | tf_op jit(solution)/shard_map/psum | solution.py:30
Sparse Core Ops, SparseCore 0:
  9.2 299.6 all-gather.1
  330.1 96.4 all-reduce.2
  428.9 36.0 reduce-scatter.1
  468.0 77.6 all-reduce.4
where the time goes:
time: 559 us; the launch traced here: 558 us
  waiting for transfers between devices  470 us (84%)
  matrix products  59.1 us (11%)
  between operations  13.2 us (2%)
  local copies, waits for them, and re-layouts  10.8 us (2%)
    all_gather x1, waiting for transfers between devices, shards(): fragment = lax.all_gather(weights, 'col', axis=2, tiled=True)  302 us
    psum x1, waiting for transfers between devices, shards(): exposure = lax.psum(joined[:, :factor_cols, :], 'row')  75.1 us
    all_to_all x1, waiting for transfers between devices, shards(): lax.all_to_all(exposure, 'col', split_axis=2, concat_axis=1, tiled=True)  47.9 us
    psum x1, waiting for transfers between devices, shards(): left = lax.psum(left_part, 'col')  44.7 us
    dot_general x1, matrix products, shards(): jnp.einsum('dak,dap->dkp', weighted, fragment, preferred_element_type=jnp...  21.5 us
    dot_general x1, matrix products, shards(): jnp.einsum('dar,dap->drp', loadings, fragment, preferred_element_type=jnp...  21.1 us
  transfers between devices with their start and end apart: 5, of which 4 were waited for; matrix products, arithmetic and copies ran while one was open for 8% of the time, Pallas kernels for 0%

commit v1 on v0

v1 whole, which is shorter than its diff:
```python
import functools

import jax
import jax.numpy as jnp
from jax import lax
from jax.experimental import pallas as pl
from jax.experimental.pallas import tpu as pltpu
from jax.sharding import PartitionSpec as P

F32, BF16 = jnp.float32, jnp.bfloat16
HIGHEST = lax.Precision.HIGHEST


def by_dim(a, b, dim, precision=None):
    return lax.dot_general(
        a, b, (((dim,), (dim,)), ((), ())), precision=precision, preferred_element_type=F32
    )


def kernel(
    rows, cols, load_hbm, weight_hbm, spec_ref, fcov_hbm, out_ref,
    held, load, fcov, weighted, part, part_in, exp_rows, exp_cols, own_spec, prod, prod_in,
    w_sem, l_sem, f_sem, g_send, g_recv, p_send, p_recv,
    er_send, er_recv, ec_send, ec_recv, q_send, q_recv,
):
    days, assets, factors = load_hbm.shape
    ports = weight_hbm.shape[2]
    slab = ports * cols // rows
    half = assets // 2
    row, col = lax.axis_index("row"), lax.axis_index("col")
    near_x = col + 1 - 2 * (col % 2)
    near_y = (col + 2) % 4
    far = 3 - col

    def to_row(r):
        return {"row": r, "col": col}

    def to_col(c):
        return {"row": row, "col": c}

    def remote(src, dst, send, recv, where):
        return pltpu.make_async_remote_copy(
            src_ref=src, dst_ref=dst, send_sem=send, recv_sem=recv,
            device_id=where, device_id_type=pl.DeviceIdType.MESH,
        )

    def gather(d, lane, block):
        ref = held.at[d, block]
        if lane == 2:
            ref = held.at[d, block, pl.ds(0, half)]
        if lane == 3:
            ref = held.at[d, block, pl.ds(half, half)]
        where = near_x if lane in (0, 3) else near_y
        return remote(ref, ref, g_send.at[d, lane], g_recv.at[d, lane], to_col(where))

    def own_weights(d):
        return pltpu.make_async_copy(weight_hbm.at[d], held.at[d, col], w_sem.at[d])

    def get_load(d):
        return pltpu.make_async_copy(load_hbm.at[d], load.at[d % 2], l_sem.at[d % 2])

    def get_fcov(d):
        return pltpu.make_async_copy(fcov_hbm.at[d], fcov.at[d % 2], f_sem.at[d % 2])

    def part_copy(d, other, landed):
        return remote(
            part.at[d % 2, pl.ds(pl.multiple_of(other * slab, slab), slab)],
            part_in.at[d, landed], p_send.at[d, other], p_recv.at[d, landed], to_row(other),
        )

    def exp_row_copy(d, other, landed):
        ref = exp_rows.at[d, pl.ds(pl.multiple_of(landed * slab, slab), slab)]
        return remote(ref, ref, er_send.at[d, other], er_recv.at[d, landed], to_row(other))

    def exp_col_copy(d, other, landed):
        ref = exp_cols.at[d, landed]
        return remote(ref, ref, ec_send.at[d, other], ec_recv.at[d, landed], to_col(other))

    def prod_copy(d, other, landed):
        return remote(
            prod.at[d, other], prod_in.at[d, landed],
            q_send.at[d, other], q_recv.at[d, landed], to_col(other),
        )

    def row_peers():
        return [(row + step) % rows for step in range(1, rows)]

    def col_peers():
        return [near_x, near_y, far]

    def send_own(d):
        own_weights(d).wait()
        gather(d, 0, col).start()
        gather(d, 1, col).start()

    def pass_on(d):
        gather(d, 0, near_x).wait_recv()
        gather(d, 2, near_x).start()
        gather(d, 1, near_y).wait_recv()
        gather(d, 3, near_y).start()

    def partial_sums(d):
        slot = d % 2
        scales = spec_ref[d]
        groups = scales.shape[0]
        copies = -(-128 // groups)
        tall = jnp.concatenate([scales] * copies, axis=0).T
        for i in range(groups):
            span = pl.ds(i * 128, 128)
            block = held[d, col, span].astype(F32) * tall[:, i : i + 1]
            weighted[span] = block.astype(BF16)

        @pl.when(d >= 2)
        def _():
            for peer in row_peers():
                part_copy(d - 2, peer, row).wait_send()

        gather(d, 2, far).wait_recv()
        gather(d, 3, far).wait_recv()
        get_load(d).wait()

        def block(j, carry):
            lhs = held[d, j]
            span = pl.ds(pl.multiple_of(j * ports, ports), ports)
            part[slot, span, pl.ds(0, factors)] = by_dim(lhs, load[slot], 0)
            part[slot, span, pl.ds(factors, ports)] = by_dim(lhs, weighted[...], 0)
            return carry

        lax.fori_loop(0, cols, block, 0)
        for peer in row_peers():
            part_copy(d, peer, row).start()
        part_in[d, row] = part[slot, pl.ds(pl.multiple_of(row * slab, slab), slab)]

        @pl.when(d + 2 < days)
        def _():
            get_load(d + 2).start()

    def exposures(d):
        for peer in row_peers():
            part_copy(d, row, peer).wait_recv()
        total = part_in[d, 0]
        for r in range(1, rows):
            total = total + part_in[d, r]
        own_spec[d] = total[:, factors:]
        exp_rows[d, pl.ds(pl.multiple_of(row * slab, slab), slab)] = total[:, :factors]
        exp_cols[d, col] = total[:, :factors]
        for peer in col_peers():
            exp_col_copy(d, peer, col).start()
        for peer in row_peers():
            exp_row_copy(d, peer, row).start()

    def products(d):
        slot = d % 2
        get_fcov(d).wait()
        for peer in col_peers():
            exp_col_copy(d, col, peer).wait_recv()
        left = jnp.zeros((slab, factors), F32)
        for j in range(cols):
            left = left + by_dim(
                exp_cols[d, j], fcov[slot, :, pl.ds(j * factors, factors)], 1, HIGHEST
            )

        @pl.when(d + 2 < days)
        def _():
            get_fcov(d + 2).start()

        for peer in row_peers():
            exp_row_copy(d, row, peer).wait_recv()
        for j in range(cols):
            prod[d, j] = by_dim(left, exp_rows[d, pl.ds(j * ports, ports)], 1, HIGHEST)
        for peer in col_peers():
            prod_copy(d, peer, col).start()
        prod_in[d, col] = prod[d, col]

    def finish(d):
        for peer in col_peers():
            prod_copy(d, col, peer).wait_recv()
        total = own_spec[d]
        for j in range(cols):
            total = total + prod_in[d, j]
        out_ref[d] = total

    for d in range(days):
        own_weights(d).start()
    for d in range(min(2, days)):
        get_load(d).start()
        get_fcov(d).start()

    barrier = pltpu.get_barrier_semaphore()
    for peer in row_peers():
        pl.semaphore_signal(
            barrier, inc=1, device_id=to_row(peer), device_id_type=pl.DeviceIdType.MESH
        )
    for peer in col_peers():
        pl.semaphore_signal(
            barrier, inc=1, device_id=to_col(peer), device_id_type=pl.DeviceIdType.MESH
        )
    pl.semaphore_wait(barrier, rows + cols - 2)

    send_own(0)
    if days > 1:
        send_own(1)

    def turn(t, carry):
        def stage(lag, what):
            @pl.when((t >= lag) & (t - lag < days))
            def _():
                what(t - lag)

        @pl.when(t + 2 < days)
        def _():
            send_own(t + 2)

        stage(0, pass_on)
        stage(2, exposures)
        stage(3, products)
        stage(4, finish)
        stage(1, partial_sums)
        return carry

    lax.fori_loop(0, days + 4, turn, 0)

    def drain(d, carry):
        gather(d, 0, col).wait_send()
        gather(d, 1, col).wait_send()
        gather(d, 2, near_x).wait_send()
        gather(d, 3, near_y).wait_send()
        for peer in row_peers():
            exp_row_copy(d, peer, row).wait_send()
        for peer in col_peers():
            exp_col_copy(d, peer, col).wait_send()
            prod_copy(d, peer, col).wait_send()

        @pl.when(d >= days - 2)
        def _():
            for peer in row_peers():
                part_copy(d, peer, row).wait_send()

        return carry

    lax.fori_loop(0, days, drain, 0)


def fused(loadings, weights, specific, factor_cov):
    rows, cols = lax.axis_size("row"), lax.axis_size("col")
    days, assets, factors = loadings.shape
    ports = weights.shape[2]
    slab = ports * cols // rows
    scales = specific.reshape(days, assets // 128, 128)
    anywhere = pl.BlockSpec(memory_space=pl.ANY)
    inside = pl.BlockSpec(memory_space=pltpu.VMEM)
    dma = pltpu.SemaphoreType.DMA
    return pl.pallas_call(
        functools.partial(kernel, rows, cols),
        out_shape=jax.ShapeDtypeStruct((days, slab, ports), F32),
        in_specs=[anywhere, anywhere, inside, anywhere],
        out_specs=inside,
        scratch_shapes=[
            pltpu.VMEM((days, cols, assets, ports), BF16),
            pltpu.VMEM((2, assets, factors), BF16),
            pltpu.VMEM((2, factors, cols * factors), F32),
            pltpu.VMEM((assets, ports), BF16),
            pltpu.VMEM((2, cols * ports, factors + ports), F32),
            pltpu.VMEM((days, rows, slab, factors + ports), F32),
            pltpu.VMEM((days, cols * ports, factors), F32),
            pltpu.VMEM((days, cols, slab, factors), F32),
            pltpu.VMEM((days, slab, ports), F32),
            pltpu.VMEM((days, cols, slab, ports), F32),
            pltpu.VMEM((days, cols, slab, ports), F32),
            dma((days,)), dma((2,)), dma((2,)),
            dma((days, 4)), dma((days, 4)),
            dma((days, rows)), dma((days, rows)),
            dma((days, rows)), dma((days, rows)),
            dma((days, cols)), dma((days, cols)),
            dma((days, cols)), dma((days, cols)),
        ],
        compiler_params=pltpu.CompilerParams(
            collective_id=0, has_side_effects=True, vmem_limit_bytes=67_000_000
        ),
        name="covariance",
    )(loadings, weights, scales, factor_cov)


def plain(loadings, weights, specific, factor_cov):
    factor_cols = loadings.shape[2]
    port_cols = weights.shape[2]
    total_ports = port_cols * lax.axis_size("col")
    port_rows = total_ports // lax.axis_size("row")
    row_start = lax.axis_index("row") * port_rows
    weighted = (specific[:, :, None] * weights.astype(F32)).astype(BF16)
    fragment = lax.all_gather(weights, "col", axis=2, tiled=True)
    exposure_part = jnp.einsum("dar,dap->drp", loadings, fragment, preferred_element_type=F32)
    specific_term = jnp.einsum("dak,dap->dkp", weighted, fragment, preferred_element_type=F32)
    joined = jnp.concatenate([exposure_part, specific_term], axis=1)
    exposure = lax.psum(joined[:, :factor_cols, :], "row")
    specific_block = lax.psum_scatter(
        joined[:, factor_cols:, :], "row", scatter_dimension=2, tiled=True
    )
    exposure_rows = lax.dynamic_slice_in_dim(exposure, row_start, port_rows, 2)
    left_part = jnp.einsum("dri,drs->dis", exposure_rows, factor_cov, precision=HIGHEST)
    left = lax.psum(left_part, "col")
    exposure_cols = lax.all_to_all(exposure, "col", split_axis=2, concat_axis=1, tiled=True)
    factor_block = jnp.einsum("dir,drk->dik", left, exposure_cols, precision=HIGHEST)
    return factor_block + jnp.swapaxes(specific_block, 1, 2)


def solution(mesh):
    in_specs = (P(None, "row", "col"), P(None, "row", "col"), P(None, "row"), P(None, "col", None))
    out_specs = P(None, "row", "col")
    body = fused if mesh.shape["col"] == 4 else plain
    return jax.shard_map(body, mesh=mesh, in_specs=in_specs, out_specs=out_specs, check_vma=False)
```

time: 559 us -> 376 us (0.67)
  waiting for transfers between devices: 470 us -> 0 us
  Pallas kernels: 0 us -> 371 us
  matrix products: 59.1 us -> 0 us
  between operations: 13.2 us -> 0.01 us
  local copies, waits for them, and re-layouts: 10.8 us -> 3.26 us
    pallas_call x0 -> x1, Pallas kernels: none -> 371 us  [fused(): pl.pallas_call(functools.partial(kernel, rows, cols), out_shape=jax.Shape...]
    all_gather x1 -> x0, waiting for transfers between devices: 302 us -> none  [shards(): fragment = lax.all_gather(weights, 'col', axis=2, tiled=True)]
    psum x2 -> x0, waiting for transfers between devices: 120 us -> none  [the longest x1 75.1 us: shards(): exposure = lax.psum(joined[:, :factor_cols, :], 'row')]
    dot_general x4 -> x0, matrix products: 59.1 us -> none  [the longest x1 21.5 us: shards(): jnp.einsum('dak,dap->dkp', weighted, fragment, preferred_element_type=jnp...]
    all_to_all x1 -> x0, waiting for transfers between devices: 47.9 us -> none  [shards(): lax.all_to_all(exposure, 'col', split_axis=2, concat_axis=1, tiled=True)]
  transfers between devices with their start and end apart: 5 -> 0, of which waited for: 4 -> 0; matrix products, arithmetic and copies ran while one was open for 8% -> 0% of each run, Pallas kernels for 0% -> 0%
where the time goes in v1:
time: 376 us; the launch traced here: 374 us
  Pallas kernels  371 us (99%)
    pallas_call x1, Pallas kernels, fused(): pl.pallas_call(functools.partial(kernel, rows, cols), out_shape=jax.Shape...  371 us

profile of v1, /device:TPU:0, one launch (start us, length us, event | category | flops | bytes accessed | tf_op | source)
XLA Modules:
  0.0 374.2 jit_solution(7237394428765055655)
XLA Ops:
  0.0 1.6 copy.7
  1.6 371.0 %covariance.1 = f32[8,64,128]{2,1,0:T(8,128)} custom-call(bf16[8,4096,256]{2,1,0:T(8,128)(2,1)} %load_hbm.1, bf16[8,4096,128]{2,1,0:T(8,128)(2,1)} %weight_hbm.1, f32[8,32,128]{2,1,0:T(8,128)} %bitcast.4, f32[8,256,1024]{2,1,0:T(8,128)} %fcov_hbm.1), custom_call_target="tpu_custom_call" | custom-call | tf_op jit(solution)/shard_map/covariance/pallas_call | solution.py:253
  372.6 1.7 copy.9

commit v2 on v1

v2 whole, which is shorter than its diff:
```python
import functools

import jax
import jax.numpy as jnp
from jax import lax
from jax.experimental import pallas as pl
from jax.experimental.pallas import tpu as pltpu
from jax.sharding import PartitionSpec as P

F32, BF16 = jnp.float32, jnp.bfloat16
HIGHEST = lax.Precision.HIGHEST
CUTS, AHEAD = 4, 2
LAGS = (4, 5, 7, 9, 12, 15)


def by_dim(a, b, dim, precision=None):
    return lax.dot_general(
        a, b, (((dim,), (dim,)), ((), ())), precision=precision, preferred_element_type=F32
    )


def kernel(
    rows, cols, cuts, load_hbm, weight_hbm, spec_ref, fcov_hbm, out_ref,
    held, load, fcov, weighted, part, mate_in, pair, part_in, exp_rows, exp_cols, own_spec, prod, prod_in,
    w_sem, l_sem, f_sem, g_send, g_recv, m_send, m_recv, p_send, p_recv,
    er_send, er_recv, ec_send, ec_recv, q_send, q_recv,
):
    days, assets, factors = load_hbm.shape
    ports = weight_hbm.shape[2]
    slab = ports * cols // rows
    row, col = lax.axis_index("row"), lax.axis_index("col")
    near_x = col + 1 - 2 * (col % 2)
    near_y = (col + 2) % 4
    far = 3 - col
    chips, per = rows // 2, rows // cols
    piece = assets // cuts
    mine, core = row // 2, row % 2
    mate = row + 1 - 2 * core

    def to_row(r):
        return {"row": r, "col": col}

    def to_col(c):
        return {"row": row, "col": c}

    def remote(src, dst, send, recv, where):
        return pltpu.make_async_remote_copy(
            src_ref=src, dst_ref=dst, send_sem=send, recv_sem=recv,
            device_id=where, device_id_type=pl.DeviceIdType.MESH,
        )

    def lanes(buf, send, recv, d, u, start, size, lane, block):
        half = size // 2
        if lane == 2:
            size = half
        if lane == 3:
            start, size = start + half, half
        ref = buf.at[d, block, pl.ds(start, size)]
        where = near_x if lane in (0, 3) else near_y
        return remote(ref, ref, send.at[u, lane], recv.at[u, lane], to_col(where))

    def gather(u, lane, block):
        start = pl.multiple_of((u % cuts) * piece, piece)
        return lanes(held, g_send, g_recv, u // cuts, u, start, piece, lane, block)

    def exp_gather(d, lane, block):
        return lanes(exp_cols, ec_send, ec_recv, d, d, 0, slab, lane, block)

    def own_weights(d):
        return pltpu.make_async_copy(weight_hbm.at[d], held.at[d, col], w_sem.at[d])

    def get_load(d):
        return pltpu.make_async_copy(load_hbm.at[d], load.at[d % 2], l_sem.at[d % 2])

    def get_fcov(d):
        return pltpu.make_async_copy(fcov_hbm.at[d], fcov.at[d % 2], f_sem.at[d % 2])

    def mate_copy(d):
        return remote(
            part.at[d % 2, 1 - core], mate_in.at[d], m_send.at[d], m_recv.at[d], to_row(mate)
        )

    def part_copy(d, other, landed):
        return remote(
            pair.at[d % 2, other], part_in.at[d, landed],
            p_send.at[d, other], p_recv.at[d, landed], to_row(2 * other + core),
        )

    def exp_row_copy(d, slot, landed, other):
        ref = exp_rows.at[d, pl.ds(pl.multiple_of(landed * slab, slab), slab)]
        return remote(ref, ref, er_send.at[d, slot], er_recv.at[d, landed], to_row(other))

    def prod_copy(d, other, landed):
        return remote(
            prod.at[d, other], prod_in.at[d, landed],
            q_send.at[d, other], q_recv.at[d, landed], to_col(other),
        )

    def row_peers():
        return [(row + step) % rows for step in range(1, rows)]

    def chip_peers():
        return [(mine + step) % chips for step in range(1, chips)]

    def col_peers():
        return [near_x, near_y, far]

    def send_own(u):
        @pl.when(u % cuts == 0)
        def _():
            own_weights(u // cuts).wait()

        gather(u, 0, col).start()
        gather(u, 1, col).start()

    def pass_on(u):
        gather(u, 0, near_x).wait_recv()
        gather(u, 2, near_x).start()
        gather(u, 1, near_y).wait_recv()
        gather(u, 3, near_y).start()

    def sum_block(d, j):
        slot = d % 2
        lhs = held[d, j]
        by_factor = by_dim(lhs, load[slot], 0)
        by_port = by_dim(lhs, weighted[...], 0)
        for i in range(per):
            span = slice(i * slab, (i + 1) * slab)
            place = j * (per // 2) + i // 2
            part[slot, i % 2, place, :, pl.ds(0, factors)] = by_factor[span]
            part[slot, i % 2, place, :, pl.ds(factors, ports)] = by_port[span]

    def near_sums(d):
        scales = spec_ref[d]
        groups = scales.shape[0]
        copies = -(-128 // groups)
        tall = jnp.concatenate([scales] * copies, axis=0).T
        for i in range(groups):
            span = pl.ds(i * 128, 128)
            block = held[d, col, span].astype(F32) * tall[:, i : i + 1]
            weighted[span] = block.astype(BF16)

        @pl.when(d >= 2)
        def _():
            mate_copy(d - 2).wait_send()
            for peer in chip_peers():
                part_copy(d - 2, peer, mine).wait_send()

        get_load(d).wait()

        def near_block(i, carry):
            sum_block(d, (far + 1 + i) % cols)
            return carry

        lax.fori_loop(0, cols - 1, near_block, 0)

    def far_sums(d):
        slot = d % 2
        for q in range(cuts):
            gather(d * cuts + q, 2, far).wait_recv()
            gather(d * cuts + q, 3, far).wait_recv()
        sum_block(d, far)
        mate_copy(d).start()

        @pl.when(d + 2 < days)
        def _():
            get_load(d + 2).start()

        mate_copy(d).wait_recv()
        for peer in chip_peers():
            pair[slot, peer] = part[slot, core, peer] + mate_in[d, peer]
            part_copy(d, peer, mine).start()
        part_in[d, mine] = part[slot, core, mine] + mate_in[d, mine]

    def exposures(d):
        for peer in chip_peers():
            part_copy(d, mine, peer).wait_recv()
        total = part_in[d, 0]
        for z in range(1, chips):
            total = total + part_in[d, z]
        own_spec[d] = total[:, factors:]
        exp_rows[d, pl.ds(pl.multiple_of(row * slab, slab), slab)] = total[:, :factors]
        exp_cols[d, col] = total[:, :factors]
        exp_gather(d, 0, col).start()
        exp_gather(d, 1, col).start()
        for peer in chip_peers():
            exp_row_copy(d, 2 * peer + core, row, 2 * peer + core).start()
        exp_row_copy(d, mate, row, mate).start()

    def share(d):
        exp_gather(d, 0, near_x).wait_recv()
        exp_gather(d, 2, near_x).start()
        exp_gather(d, 1, near_y).wait_recv()
        exp_gather(d, 3, near_y).start()
        for peer in chip_peers():
            exp_row_copy(d, row, 2 * peer + core, mate).wait_recv()
            exp_row_copy(d, 2 * peer + 1 - core, 2 * peer + core, mate).start()

    def products(d):
        slot = d % 2
        get_fcov(d).wait()
        exp_gather(d, 2, far).wait_recv()
        exp_gather(d, 3, far).wait_recv()
        left = jnp.zeros((slab, factors), F32)
        for j in range(cols):
            left = left + by_dim(
                exp_cols[d, j], fcov[slot, :, pl.ds(j * factors, factors)], 1, HIGHEST
            )

        @pl.when(d + 2 < days)
        def _():
            get_fcov(d + 2).start()

        exp_row_copy(d, row, mate, mate).wait_recv()
        for peer in chip_peers():
            exp_row_copy(d, row, 2 * peer + 1 - core, mate).wait_recv()
        for j in range(cols):
            prod[d, j] = by_dim(left, exp_rows[d, pl.ds(j * ports, ports)], 1, HIGHEST)
        for peer in col_peers():
            prod_copy(d, peer, col).start()
        prod_in[d, col] = prod[d, col]

    def finish(d):
        for peer in col_peers():
            prod_copy(d, col, peer).wait_recv()
        total = own_spec[d]
        for j in range(cols):
            total = total + prod_in[d, j]
        out_ref[d] = total

    for d in range(days):
        own_weights(d).start()
    for d in range(min(2, days)):
        get_load(d).start()
        get_fcov(d).start()

    barrier = pltpu.get_barrier_semaphore()
    for peer in row_peers():
        pl.semaphore_signal(
            barrier, inc=1, device_id=to_row(peer), device_id_type=pl.DeviceIdType.MESH
        )
    for peer in col_peers():
        pl.semaphore_signal(
            barrier, inc=1, device_id=to_col(peer), device_id_type=pl.DeviceIdType.MESH
        )
    pl.semaphore_wait(barrier, rows + cols - 2)

    for u in range(AHEAD):
        send_own(u)

    def turn(t, carry):
        def stage(lag, what):
            @pl.when((t >= lag) & ((t - lag) % cuts == 0) & (t - lag < cuts * days))
            def _():
                what((t - lag) // cuts)

        @pl.when(t + AHEAD < cuts * days)
        def _():
            send_own(t + AHEAD)

        @pl.when(t < cuts * days)
        def _():
            pass_on(t)

        for lag, what in zip(LAGS, (near_sums, far_sums, exposures, share, products, finish)):
            stage(lag, what)
        return carry

    lax.fori_loop(0, cuts * (days - 1) + LAGS[-1] + 1, turn, 0)

    def drain(d, carry):
        for u in range(cuts):
            gather(d * cuts + u, 0, col).wait_send()
            gather(d * cuts + u, 1, col).wait_send()
            gather(d * cuts + u, 2, near_x).wait_send()
            gather(d * cuts + u, 3, near_y).wait_send()
        exp_gather(d, 0, col).wait_send()
        exp_gather(d, 1, col).wait_send()
        exp_gather(d, 2, near_x).wait_send()
        exp_gather(d, 3, near_y).wait_send()
        exp_row_copy(d, mate, row, mate).wait_send()
        for peer in chip_peers():
            exp_row_copy(d, 2 * peer + core, row, 2 * peer + core).wait_send()
            exp_row_copy(d, 2 * peer + 1 - core, 2 * peer + core, mate).wait_send()
        for peer in col_peers():
            prod_copy(d, peer, col).wait_send()

        @pl.when(d >= days - 2)
        def _():
            mate_copy(d).wait_send()
            for peer in chip_peers():
                part_copy(d, peer, mine).wait_send()

        return carry

    lax.fori_loop(0, days, drain, 0)


def fused(loadings, weights, specific, factor_cov):
    rows, cols = lax.axis_size("row"), lax.axis_size("col")
    days, assets, factors = loadings.shape
    ports = weights.shape[2]
    slab = ports * cols // rows
    scales = specific.reshape(days, assets // 128, 128)
    anywhere = pl.BlockSpec(memory_space=pl.ANY)
    inside = pl.BlockSpec(memory_space=pltpu.VMEM)
    dma = pltpu.SemaphoreType.DMA
    return pl.pallas_call(
        functools.partial(kernel, rows, cols, CUTS),
        out_shape=jax.ShapeDtypeStruct((days, slab, ports), F32),
        in_specs=[anywhere, anywhere, inside, anywhere],
        out_specs=inside,
        scratch_shapes=[
            pltpu.VMEM((days, cols, assets, ports), BF16),
            pltpu.VMEM((2, assets, factors), BF16),
            pltpu.VMEM((2, factors, cols * factors), F32),
            pltpu.VMEM((assets, ports), BF16),
            pltpu.VMEM((2, 2, rows // 2, slab, factors + ports), F32),
            pltpu.VMEM((days, rows // 2, slab, factors + ports), F32),
            pltpu.VMEM((2, rows // 2, slab, factors + ports), F32),
            pltpu.VMEM((days, rows // 2, slab, factors + ports), F32),
            pltpu.VMEM((days, cols * ports, factors), F32),
            pltpu.VMEM((days, cols, slab, factors), F32),
            pltpu.VMEM((days, slab, ports), F32),
            pltpu.VMEM((days, cols, slab, ports), F32),
            pltpu.VMEM((days, cols, slab, ports), F32),
            dma((days,)), dma((2,)), dma((2,)),
            dma((days * CUTS, 4)), dma((days * CUTS, 4)),
            dma((days,)), dma((days,)),
            dma((days, rows // 2)), dma((days, rows // 2)),
            dma((days, rows)), dma((days, rows)),
            dma((days, cols)), dma((days, cols)),
            dma((days, cols)), dma((days, cols)),
        ],
        compiler_params=pltpu.CompilerParams(
            collective_id=0, has_side_effects=True, vmem_limit_bytes=67_000_000
        ),
        name="covariance",
    )(loadings, weights, scales, factor_cov)


def plain(loadings, weights, specific, factor_cov):
    factor_cols = loadings.shape[2]
    port_cols = weights.shape[2]
    total_ports = port_cols * lax.axis_size("col")
    port_rows = total_ports // lax.axis_size("row")
    row_start = lax.axis_index("row") * port_rows
    weighted = (specific[:, :, None] * weights.astype(F32)).astype(BF16)
    fragment = lax.all_gather(weights, "col", axis=2, tiled=True)
    exposure_part = jnp.einsum("dar,dap->drp", loadings, fragment, preferred_element_type=F32)
    specific_term = jnp.einsum("dak,dap->dkp", weighted, fragment, preferred_element_type=F32)
    joined = jnp.concatenate([exposure_part, specific_term], axis=1)
    exposure = lax.psum(joined[:, :factor_cols, :], "row")
    specific_block = lax.psum_scatter(
        joined[:, factor_cols:, :], "row", scatter_dimension=2, tiled=True
    )
    exposure_rows = lax.dynamic_slice_in_dim(exposure, row_start, port_rows, 2)
    left_part = jnp.einsum("dri,drs->dis", exposure_rows, factor_cov, precision=HIGHEST)
    left = lax.psum(left_part, "col")
    exposure_cols = lax.all_to_all(exposure, "col", split_axis=2, concat_axis=1, tiled=True)
    factor_block = jnp.einsum("dir,drk->dik", left, exposure_cols, precision=HIGHEST)
    return factor_block + jnp.swapaxes(specific_block, 1, 2)


def solution(mesh):
    in_specs = (P(None, "row", "col"), P(None, "row", "col"), P(None, "row"), P(None, "col", None))
    out_specs = P(None, "row", "col")
    rows, cols = mesh.shape["row"], mesh.shape["col"]
    body = fused if cols == 4 and rows % (2 * cols) == 0 else plain
    return jax.shard_map(body, mesh=mesh, in_specs=in_specs, out_specs=out_specs, check_vma=False)
```

time: 376 us -> 331 us (0.88)
  Pallas kernels: 371 us -> 327 us
    pallas_call x1, Pallas kernels: 371 us -> 327 us  [fused(): pl.pallas_call(functools.partial(kernel, rows, cols, CUTS), out_shape=jax...]
where the time goes in v2:
time: 331 us
  Pallas kernels  327 us (99%)
    pallas_call x1, Pallas kernels, fused(): pl.pallas_call(functools.partial(kernel, rows, cols, CUTS), out_shape=jax...  327 us

profile of v2, /device:TPU:0, one launch (start us, length us, event | category | flops | bytes accessed | tf_op | source)
XLA Modules:
  0.0 330.7 jit_solution(6472951391445066049)
XLA Ops:
  0.0 1.6 copy.7
  1.6 327.4 %covariance.1 = f32[8,64,128]{2,1,0:T(8,128)} custom-call(bf16[8,4096,256]{2,1,0:T(8,128)(2,1)} %load_hbm.1, bf16[8,4096,128]{2,1,0:T(8,128)(2,1)} %weight_hbm.1, f32[8,32,128]{2,1,0:T(8,128)} %bitcast.4, f32[8,256,1024]{2,1,0:T(8,128)} %fcov_hbm.1), custom_call_target="tpu_custom_call" | custom-call | tf_op jit(solution)/shard_map/covariance/pallas_call | solution.py:308
  329.0 1.7 copy.9
